TPU v7x, 32 devices: a whole 2x2x4 slice. The times are simulated.
32 devices in a mesh: gx: 4 (over z), gy: 4 (over x, core), col: 2 (over y).
Axes of the slice: x: 2, y: 2, z: 4, core: 2. Of those that a mesh axis runs over, the one named last changes fastest.
Arguments:
- fields: bfloat16 [2, 128, 128, 32, 128], P('col', 'gx', 'gy'), may hold values from -6 to 6
- spectral: bfloat16 [1, 16, 16, 2, 32, 32, 16], P(None, 'gx', 'gy', None, None, 'col'), may hold values from -0.75 to 0.75
- skip_weight: bfloat16 [1, 32, 32], replicated, may hold values from -1 to 1
- skip_bias: float32 [1, 32], replicated, may hold values from -3 to 3
- norm_gain: float32 [1, 32], replicated, may hold values from 0.5 to 1.5
- norm_shift: float32 [1, 32], replicated, may hold values from -3 to 3
Outputs:
- activations: bfloat16 [2, 128, 128, 32, 128], P('col', 'gx', 'gy')
All inputs are finite; a program needn't handle non-finite values.
Results may differ from a plain program's by a relative error of at most 0.012.
Values may be sent and summed in bfloat16 or wider, within the bound.
A program may use at most 128 MiB of HBM per device.

v0:
```python
import math
import jax
import jax.numpy as jnp
from jax import lax
from jax.sharding import PartitionSpec as P

X = 128
Y = 128
Z = 128
MX = 16
MY = 16
MZ = 16
norm_eps = 1e-05


def signed_freqs(count):
    index = jnp.arange(count, dtype=jnp.int32)
    return jnp.where(index < count // 2, index, index - count)


def angles(positions, frequency, length):
    turn_count = positions[:, None] * frequency[None, :] % length
    return turn_count.astype(jnp.float32) * (2.0 * math.pi / length)


def forward_table(positions, frequency, length, factor):
    phase_angle = angles(positions, frequency, length)
    cosine = jnp.cos(phase_angle) * factor
    sine_part = jnp.sin(phase_angle) * factor
    from_real = jnp.stack([cosine, -sine_part], axis=-1)
    from_imag = jnp.stack([sine_part, cosine], axis=-1)
    return jnp.stack([from_real, from_imag], axis=1)


def inverse_table(frequency, positions, length):
    phase_angle = angles(positions, frequency, length).T
    cosine = jnp.cos(phase_angle)
    sine_part = jnp.sin(phase_angle)
    from_real = jnp.stack([cosine, sine_part], axis=-1)
    from_imag = jnp.stack([-sine_part, cosine], axis=-1)
    return jnp.stack([from_real, from_imag], axis=1)


def depth_tables(length, count):
    frequency = jnp.arange(count, dtype=jnp.int32)
    phase_angle = angles(jnp.arange(length, dtype=jnp.int32), frequency, length)
    forward = jnp.concatenate([jnp.cos(phase_angle), -jnp.sin(phase_angle)], axis=1)
    backward = jnp.concatenate([jnp.cos(phase_angle).T, -jnp.sin(phase_angle).T], axis=0)
    return (forward.astype(jnp.bfloat16), backward.astype(jnp.bfloat16))


def mix_modes(spectrum, weight):

    def contract(left, right):
        return jnp.einsum("abcz,abcdz->abdz", left, right, preferred_element_type=jnp.float32)

    real_in = spectrum[:, :, :, 0]
    imag_in = spectrum[:, :, :, 1]
    real_weight = weight[:, :, 0]
    imag_weight = weight[:, :, 1]
    real_out = contract(real_in, real_weight) - contract(imag_in, imag_weight)
    imag_out = contract(real_in, imag_weight) + contract(imag_in, real_weight)
    return jnp.stack([real_out, imag_out], axis=3)


def finish(spectral_part, skip_part, offset, scaling, shift_term):
    pre_norm = spectral_part + skip_part + offset[:, None]
    centre = jnp.mean(pre_norm, axis=2, keepdims=True)
    spread = jnp.mean(jnp.square(pre_norm - centre), axis=2, keepdims=True)
    normed = (pre_norm - centre) * lax.rsqrt(spread + norm_eps) * scaling[:, None] + shift_term[
        :, None
    ]
    return jax.nn.gelu(normed, approximate=False).astype(jnp.bfloat16)


def local(fields, spectral, skip_weight, skip_bias, norm_gain, norm_shift):
    highest = lax.Precision.HIGHEST
    hidden = fields[0]
    tile_first, tile_second, channels, depth_cells = hidden.shape
    first_cells = lax.axis_index("gx") * tile_first + jnp.arange(tile_first, dtype=jnp.int32)
    second_cells = lax.axis_index("gy") * tile_second + jnp.arange(tile_second, dtype=jnp.int32)
    depth_forward, depth_backward = depth_tables(Z, MZ)
    second_forward = forward_table(second_cells, signed_freqs(MY), Y, 1.0).astype(jnp.bfloat16)
    first_forward = forward_table(first_cells, signed_freqs(MX), X, 1.0 / math.sqrt(X * Y * Z))
    first_inverse = inverse_table(signed_freqs(MX), first_cells, X).astype(jnp.bfloat16)
    second_inverse = inverse_table(signed_freqs(MY), second_cells, Y)
    inverse_scale = 1.0 / math.sqrt(MX * MY * MZ)
    amplitude = jnp.dot(
        hidden.reshape(-1, depth_cells), depth_forward, preferred_element_type=jnp.float32
    )
    amplitude = amplitude.astype(jnp.bfloat16).reshape(tile_first, tile_second, channels, 2, MZ)
    along_second = jnp.einsum(
        "xycrz,yrks->xkcsz", amplitude, second_forward, preferred_element_type=jnp.float32
    )
    summed_second = lax.psum_scatter(
        along_second.astype(jnp.bfloat16), "gy", scatter_dimension=1, tiled=True
    ).astype(jnp.float32)
    partial_modes = jnp.einsum("xkcsz,xsjt->jkctz", summed_second, first_forward, precision=highest)
    summed = lax.psum_scatter(
        partial_modes.astype(jnp.bfloat16), "gx", scatter_dimension=0, tiled=True
    )
    weights_here = spectral[0]
    mixed_modes = mix_modes(summed, lax.all_gather(weights_here, "col", axis=4, tiled=True)).astype(
        jnp.bfloat16
    )
    gathered_second = lax.all_gather(mixed_modes, "gy", axis=1, tiled=True)
    full_modes = lax.all_gather(gathered_second, "gx", axis=0, tiled=True)
    rows_first = jnp.einsum(
        "jkcsz,jsxt->xkctz", full_modes, first_inverse, preferred_element_type=jnp.float32
    )
    rows_both = jnp.einsum(
        "xkcsz,ksyt->xyctz", rows_first, second_inverse, precision=highest
    ).astype(jnp.bfloat16)
    spectral_part = jnp.dot(
        rows_both.reshape(-1, 2 * MZ), depth_backward, preferred_element_type=jnp.float32
    )
    spectral_part = (
        spectral_part.reshape(tile_first, tile_second, channels, depth_cells) * inverse_scale
    )
    skip_part = jnp.einsum(
        "oc,xycz->xyoz", skip_weight[0], hidden, preferred_element_type=jnp.float32
    )
    hidden = finish(spectral_part, skip_part, skip_bias[0], norm_gain[0], norm_shift[0])
    return hidden[None]


def solution(mesh):
    placed = (
        P("col", "gx", "gy", None, None),
        P(None, "gx", "gy", None, None, "col", None),
        P(),
        P(),
        P(),
        P(),
    )
    return jax.shard_map(
        local,
        mesh=mesh,
        in_specs=placed,
        out_specs=P("col", "gx", "gy", None, None),
        check_vma=False,
    )
```

profile of v0, /device:TPU:0, one launch (start us, length us, event | category | flops | bytes accessed | tf_op | source)
XLA Modules:
  0.0 268.1 jit_solution(5952482807343169716)
XLA Ops:
  7.4 6.4 %fusion = bf16[32768,32]{0,1:T(8,128)(2,1)S(1)} fusion(bf16[32768,128]{1,0:T(8,128)(2,1)} %bitcast.159, bf16[128,16]{0,1:T(8,128)(2,1)S(1)} %get-tuple-element.37, bf16[128,16]{0,1:T(8,128)(2,1)S(1)} %get-tuple-element.38), kind=kOutput, calls=%fused_computation.1 | convolution fusion | flops 269500416 | bytes 10493952 | tf_op jit(solution)/shard_map/dot_general | solution.py:88
  13.8 7.9 %reshape.722 = bf16[32,32,32,2,16]{2,1,0,4,3:T(8,128)(2,1)} reshape(bf16[32768,32]{0,1:T(8,128)(2,1)S(1)} %fusion) | data formatting | bytes 4194304 | tf_op jit(solution)/shard_map/reshape | solution.py:91
  21.9 4.7 %fusion.24 = bf16[32,16,32,2,16]{2,1,4,0,3:T(8,128)(2,1)S(1)} fusion(bf16[32,32,32,2,16]{2,1,0,4,3:T(8,128)(2,1)} %reshape.722, bf16[32,1,16,2]{0,2,1,3:T(8,128)(2,1)S(1)} %get-tuple-element.16, bf16[32,1,16,2]{0,2,1,3:T(8,128)(2,1)S(1)} %get-tuple-element.15), kind=kOutput, calls=%fused_computation.37 | convolution fusion | flops 67641344 | bytes 3149824 | tf_op jit(solution)/shard_map/xycrz,yrks->xkcsz/dot_general | solution.py:92
  26.6 3.1 %copy.26 = bf16[32,16,32,2,16]{2,4,3,0,1:T(8,128)(2,1)} copy(bf16[32,16,32,2,16]{2,1,4,0,3:T(8,128)(2,1)S(1)} %fusion.24) | data formatting | bytes 2097152 | tf_op jit(solution)/shard_map/convert_element_type | solution.py:96
  30.8 15.1 %fusion.13 = f32[32,32,128,32]{2,3,1,0:T(8,128)} fusion(bf16[1,32,32,32,128]{4,3,2,1,0:T(8,128)(2,1)} %param.6, bf16[1,32,32]{2,1,0:T(8,128)(2,1)S(1)} %copy-done), kind=kOutput, calls=%fused_computation.27 | convolution fusion | flops 268435456 | bytes 25167872 | tf_op jit(solution)/shard_map/oc,xycz->xyoz/dot_general | solution.py:120
  46.0 31.2 %reduce-scatter.3.cloned.1.call-done = bf16[32,4,32,2,16]{2,4,3,0,1:T(8,128)(2,1)} async-done(((bf16[32,16,32,2,16]{2,4,3,0,1:T(8,128)(2,1)}), bf16[32,4,32,2,16]{2,4,3,0,1:T(8,128)(2,1)}) %reduce-scatter.3.cloned.1.call-update) | async-done | bytes 262160 | tf_op jit(solution)/shard_map/reduce_scatter | solution.py:95
  77.2 1.9 fusion.30
  79.1 0.9 copy.29
  80.1 11.0 %all-gather.3.cloned.1.call-done = bf16[1,4,4,2,32,32,16]{4,6,5,3,2,1,0:T(8,128)(2,1)} async-done(((bf16[1,4,4,2,32,16,16]{4,6,5,3,2,1,0:T(8,128)(2,1)}), bf16[1,4,4,2,32,32,16]{4,6,5,3,2,1,0:T(8,128)(2,1)}) %all-gather.3.cloned.1.call-update) | async-done | bytes 1048592 | tf_op jit(solution)/shard_map/all_gather | solution.py:103
  91.1 4.5 %slice_bitcast_fusion = (bf16[4,4,32,32,16]{2,4,3,1,0:T(8,128)(2,1)}, bf16[4,4,32,32,16]{2,4,3,1,0:T(8,128)(2,1)S(1)}) fusion(bf16[4,4,2,32,32,16]{3,5,4,2,1,0:T(8,128)(2,1)} %bitcast.161), kind=kLoop, calls=%fused_computation.39 | loop fusion | bytes 2097152 | tf_op jit(solution)/shard_map/squeeze | solution.py:60
  95.6 4.5 %copy.44 = bf16[4,4,32,32,16]{3,2,4,1,0:T(8,128)(2,1)} copy(bf16[4,4,32,32,16]{2,4,3,1,0:T(8,128)(2,1)} %get-tuple-element.5) | data formatting | bytes 1048576 | tf_op jit(solution)/shard_map/squeeze | solution.py:60
  100.2 2.9 %copy.41 = bf16[4,4,32,32,16]{3,2,4,1,0:T(8,128)(2,1)} copy(bf16[4,4,32,32,16]{2,4,3,1,0:T(8,128)(2,1)S(1)} %get-tuple-element.6) | data formatting | bytes 1048576 | tf_op jit(solution)/shard_map/squeeze | solution.py:59
  104.0 2.2 fusion.39
  106.2 2.3 fusion.37
  108.5 2.3 fusion.35
  110.7 2.2 fusion.41
  113.1 7.2 %all_gather.10 = bf16[4,16,32,2,16]{2,4,3,0,1:T(8,128)(2,1)S(1)} all-gather(bf16[4,4,32,2,16]{2,4,3,0,1:T(8,128)(2,1)S(1)} %pad_maximum_fusion), channel_id=1, replica_groups=mesh['gx'=4,'gy'=4,'col'=2] {'gy'}, dimensions={1}, use_global_device_ids=true | all-gather | bytes 163840 | tf_op jit(solution)/shard_map/all_gather | solution.py:106
  120.3 38.6 %all_gather.11 = bf16[16,16,32,2,16]{2,4,3,1,0:T(8,128)(2,1)S(1)} all-gather(bf16[4,16,32,2,16]{2,4,3,1,0:T(8,128)(2,1)S(1)} %copy.30), channel_id=1, replica_groups=mesh['gx'=4,'gy'=4,'col'=2] {'gx'}, dimensions={0}, use_global_device_ids=true | all-gather | bytes 655360 | tf_op jit(solution)/shard_map/all_gather | solution.py:107
  158.8 1.5 convolution_bitcast_fusion
  160.3 22.8 %fusion.12 = bf16[32,32,32,2,16]{2,1,4,0,3:T(8,128)(2,1)} fusion(f32[32,16,32,2,16]{2,0,4,1,3:T(8,128)S(1)} %convolution_bitcast_fusion, f32[16,1,32,2]{2,0,3,1:T(8,128)S(1)} %get-tuple-element.10, f32[16,1,32,2]{2,0,3,1:T(8,128)S(1)} %get-tuple-element.9), kind=kOutput, calls=%fused_computation.26 | convolution fusion | flops 403703808 | bytes 4202496 | tf_op jit(solution)/shard_map/xkcsz,ksyt->xyctz/dot_general | solution.py:111
  183.1 10.5 %copy.34 = bf16[32,32,32,2,16]{2,4,3,1,0:T(8,128)(2,1)} copy(bf16[32,32,32,2,16]{2,1,4,0,3:T(8,128)(2,1)} %fusion.12) | data formatting | bytes 4194304 | tf_op jit(solution)/shard_map/convert_element_type | solution.py:113
  193.6 14.5 %fusion.93 = (f32[32,32,128]{2,1,0:T(8,128)S(1)}, f32[32,32,32,128]{3,2,1,0:T(8,128)}) fusion(f32[32]{0:T(128)S(1)} %bitcast.164, f32[32,32,128,32]{2,3,1,0:T(8,128)} %fusion.13, bf16[32,32,32,32]{2,3,1,0:T(8,128)(2,1)} %bitcast.160, bf16[16,128]{1,0:T(8,128)(2,1)S(1)} %get-tuple-element.41, bf16[16,128]{1,0:T(8,128)(2,1)S(1)} %get-tuple-element.42), kind=kOutput, calls=%fused_computation.167 | convolution fusion | flops 285097984 | bytes 36184192 | tf_op jit(solution)/shard_map/dot_general | solution.py:114
  208.2 10.9 %multiply_reduce_fusion = f32[32,32,128]{2,1,0:T(8,128)S(1)} fusion(f32[32,32,32,128]{3,2,1,0:T(8,128)} %get-tuple-element.36, f32[32,32,128]{2,1,0:T(8,128)S(1)} %broadcast_multiply_fusion), kind=kLoop, calls=%fused_computation.23 | loop fusion | flops 12451840 | bytes 17825792 | tf_op jit(solution)/shard_map/reduce_sum | solution.py:69
  219.2 41.4 %fusion.21 = bf16[1,32,32,32,128]{4,3,2,1,0:T(8,128)(2,1)} fusion(f32[32]{0:T(128)S(1)} %bitcast.162, f32[32]{0:T(128)S(1)} %bitcast.163, f32[32,32,128]{2,1,0:T(8,128)S(1)} %add_rsqrt_fusion, f32[32,32,32,128]{3,2,1,0:T(8,128)} %get-tuple-element.36, f32[32,32,128]{2,1,0:T(8,128)S(1)} %broadcast_multiply_fusion), kind=kLoop, calls=%fused_computation.36 | loop fusion | flops 289406976 | bytes 26214656 | tf_op jit(solution)/shard_map/broadcast_in_dim | solution.py:124
  (34 shorter events, 2.4 us)
Async XLA Ops:
  7.4 23.4 %copy-start = (bf16[1,32,32]{2,1,0:T(8,128)(2,1)S(1)}, bf16[1,32,32]{2,1,0:T(8,128)(2,1)}, u32[]{:S(2)}) copy-start(bf16[1,32,32]{2,1,0:T(8,128)(2,1)} %param.8) | copy-start | bytes 6148
  7.4 69.8 %reduce-scatter.3.cloned.1.call-start = ((), (), s32[]{:S(2)}) async-start(), calls=%async_computation.2 | async-start | bytes 5242880 | tf_op jit(solution)/shard_map/reduce_scatter | solution.py:95
  29.7 61.4 %all-gather.3.cloned.1.call-start = ((), (), s32[]{:S(2)}) async-start(), calls=%async_computation.4 | async-start | bytes 6291456 | tf_op jit(solution)/shard_map/all_gather | solution.py:103
  30.3 72.8 %reduce-scatter.5.cloned.1.call-start = ((), (), s32[]{:S(2)}) async-start(), calls=%async_computation.3 | async-start | bytes 655360 | tf_op jit(solution)/shard_map/reduce_scatter | solution.py:99
  160.3 33.3 %copy-start.4 = (f32[1,32]{1,0:T(1,128)S(1)}, f32[1,32]{1,0:T(1,128)}, u32[]{:S(2)}) copy-start(f32[1,32]{1,0:T(1,128)} %param.9) | copy-start | bytes 388
  208.1 11.1 %copy-start.2 = (f32[1,32]{1,0:T(1,128)S(1)}, f32[1,32]{1,0:T(1,128)}, u32[]{:S(2)}) copy-start(f32[1,32]{1,0:T(1,128)} %param.11) | copy-start | bytes 388
  208.1 11.1 %copy-start.3 = (f32[1,32]{1,0:T(1,128)S(1)}, f32[1,32]{1,0:T(1,128)}, u32[]{:S(2)}) copy-start(f32[1,32]{1,0:T(1,128)} %param.10) | copy-start | bytes 388
  208.2 52.5 %copy-start.1 = (bf16[1,32,32]{2,1,0:T(8,128)(2,1)S(1)}, bf16[1,32,32]{2,1,0:T(8,128)(2,1)}, u32[]{:S(2)}) copy-start(bf16[1,32,32]{2,1,0:T(8,128)(2,1)} %param.8) | copy-start | bytes 6148
Sparse Core Ops, SparseCore 0:
  29.9 47.2 reduce-scatter.2
  80.2 21.8 reduce-scatter.4
Sparse Core Ops, SparseCore 1:
  31.8 59.3 all-gather.2
where the time goes:
time: 269 us; the launch traced here: 268 us
  matrix products  75.9 us (28%)
  other arithmetic  53 us (20%)
  blocking collectives  45.7 us (17%)
  waiting for transfers between devices  42.8 us (16%)
  local copies, waits for them, and re-layouts  35.4 us (13%)
  between operations  15 us (6%)
    broadcast_in_dim x1, other arithmetic, local(): return hidden[None]  41.4 us
    all_gather x1, blocking collectives, local(): full_modes = lax.all_gather(gathered_second, 'gx', axis=0, tiled=True)  38.6 us
    reduce_scatter x1, waiting for transfers between devices, local(): lax.psum_scatter(along_second.astype(jnp.bfloat16), 'gy', scatter_dimensi...  31.2 us
    dot_general x1, matrix products, local(): jnp.einsum('xkcsz,ksyt->xyctz', rows_first, second_inverse, precision=hig...  22.8 us
    dot_general x1, matrix products, local(): jnp.einsum('oc,xycz->xyoz', skip_weight[0], hidden, preferred_element_typ...  15.1 us
    dot_general x1, matrix products, local(): jnp.dot(rows_both.reshape(-1, 2 * MZ), depth_backward, preferred_element_...  14.5 us
    all_gather x1, waiting for transfers between devices, local(): lax.all_gather(weights_here, 'col', axis=4, tiled=True)  11 us
    reduce_sum x1, other arithmetic, finish(): spread = jnp.mean(jnp.square(pre_norm - centre), axis=2, keepdims=True)  10.9 us
  transfers between devices with their start and end apart: 3, of which 2 were waited for; matrix products, arithmetic and copies ran while one was open for 11% of the time, Pallas kernels for 0%

commit v1 on v0

--- a/solution.py
+++ b/solution.py
@@ -104,7 +104,12 @@
         jnp.bfloat16
     )
     gathered_second = lax.all_gather(mixed_modes, "gy", axis=1, tiled=True)
-    full_modes = lax.all_gather(gathered_second, "gx", axis=0, tiled=True)
+    ring = [gathered_second]
+    for hop in range(3):
+        ring.append(lax.ppermute(ring[-1], "gx", [(dev, (dev + 1) % 4) for dev in range(4)]))
+    full_modes = jnp.roll(
+        jnp.concatenate(ring[::-1], axis=0), (lax.axis_index("gx") + 1) * ring[0].shape[0], axis=0
+    )
     rows_first = jnp.einsum(
         "jkcsz,jsxt->xkctz", full_modes, first_inverse, preferred_element_type=jnp.float32
     )

time: 269 us -> 290 us (1.078)
  waiting for transfers between devices: 42.8 us -> 90.5 us
  blocking collectives: 45.7 us -> 7.15 us
  local copies, waits for them, and re-layouts: 35.4 us -> 48 us
    all_gather x1 -> x0, blocking collectives: 38.6 us -> none  [local(): full_modes = lax.all_gather(gathered_second, 'gx', axis=0, tiled=True)]
    ppermute x0 -> x3, waiting for transfers between devices: none -> 32.1 us  [local(): lax.ppermute(ring[-1], 'gx', [(dev, (dev + 1) % 4) for dev in range(4)])]
    reduce_scatter x1, waiting for transfers between devices: 31.2 us -> 46.8 us  [local(): lax.psum_scatter(along_second.astype(jnp.bfloat16), 'gy', scatter_dimensi...]
    concatenate x0 -> x1, local copies, waits for them, and re-layouts: none -> 12.3 us  [local(): jnp.roll(jnp.concatenate(ring[::-1], axis=0), (lax.axis_index('gx') + 1)...]
    dot_general x1, matrix products: 15.1 us -> 11.5 us  [local(): jnp.einsum('oc,xycz->xyoz', skip_weight[0], hidden, preferred_element_typ...]
  transfers between devices with their start and end apart: 3 -> 6, of which waited for: 2 -> 5; matrix products, arithmetic and copies ran while one was open for 11% -> 9% of each run, Pallas kernels for 0% -> 0%
where the time goes in v1:
time: 290 us; the launch traced here: 289 us
  waiting for transfers between devices  90.5 us (31%)
  matrix products  73.8 us (25%)
  other arithmetic  53 us (18%)
  local copies, waits for them, and re-layouts  48 us (17%)
  between operations  15 us (5%)
  blocking collectives  7.15 us (2%)
    reduce_scatter x1, waiting for transfers between devices, local(): lax.psum_scatter(along_second.astype(jnp.bfloat16), 'gy', scatter_dimensi...  46.8 us
    broadcast_in_dim x1, other arithmetic, local(): return hidden[None]  41.4 us
    ppermute x3, waiting for transfers between devices, local(): lax.ppermute(ring[-1], 'gx', [(dev, (dev + 1) % 4) for dev in range(4)])  32.1 us
    dot_general x1, matrix products, local(): jnp.einsum('xkcsz,ksyt->xyctz', rows_first, second_inverse, precision=hig...  22.8 us
    dot_general x1, matrix products, local(): jnp.dot(rows_both.reshape(-1, 2 * MZ), depth_backward, preferred_element_...  14.5 us
    concatenate x1, local copies, waits for them, and re-layouts, local(): jnp.roll(jnp.concatenate(ring[::-1], axis=0), (lax.axis_index('gx') + 1)...  12.3 us
    dot_general x1, matrix products, local(): jnp.einsum('oc,xycz->xyoz', skip_weight[0], hidden, preferred_element_typ...  11.5 us
    all_gather x1, waiting for transfers between devices, local(): lax.all_gather(weights_here, 'col', axis=4, tiled=True)  11 us
  transfers between devices with their start and end apart: 6, of which 5 were waited for; matrix products, arithmetic and copies ran while one was open for 9% of the time, Pallas kernels for 0%

profile of v1, /device:TPU:0, one launch (start us, length us, event | category | flops | bytes accessed | tf_op | source)
XLA Modules:
  0.0 289.3 jit_solution(12933285335189747278)
XLA Ops:
  7.4 6.4 %fusion = bf16[32768,32]{0,1:T(8,128)(2,1)S(1)} fusion(bf16[32768,128]{1,0:T(8,128)(2,1)} %bitcast.159, bf16[128,16]{0,1:T(8,128)(2,1)S(1)} %get-tuple-element.37, bf16[128,16]{0,1:T(8,128)(2,1)S(1)} %get-tuple-element.38), kind=kOutput, calls=%fused_computation.1 | convolution fusion | flops 269500416 | bytes 10493952 | tf_op jit(solution)/shard_map/dot_general | solution.py:88
  13.8 7.9 %reshape.722 = bf16[32,32,32,2,16]{2,1,0,4,3:T(8,128)(2,1)} reshape(bf16[32768,32]{0,1:T(8,128)(2,1)S(1)} %fusion) | data formatting | bytes 4194304 | tf_op jit(solution)/shard_map/reshape | solution.py:91
  21.9 4.7 %fusion.24 = bf16[32,16,32,2,16]{2,1,4,0,3:T(8,128)(2,1)S(1)} fusion(bf16[32,32,32,2,16]{2,1,0,4,3:T(8,128)(2,1)} %reshape.722, bf16[32,1,16,2]{0,2,1,3:T(8,128)(2,1)S(1)} %get-tuple-element.16, bf16[32,1,16,2]{0,2,1,3:T(8,128)(2,1)S(1)} %get-tuple-element.15), kind=kOutput, calls=%fused_computation.37 | convolution fusion | flops 67641344 | bytes 3149824 | tf_op jit(solution)/shard_map/xycrz,yrks->xkcsz/dot_general | solution.py:92
  26.6 3.1 %copy.26 = bf16[32,16,32,2,16]{2,4,3,0,1:T(8,128)(2,1)} copy(bf16[32,16,32,2,16]{2,1,4,0,3:T(8,128)(2,1)S(1)} %fusion.24) | data formatting | bytes 2097152 | tf_op jit(solution)/shard_map/convert_element_type | solution.py:96
  30.4 46.8 %reduce-scatter.3.cloned.1.call-done = bf16[32,4,32,2,16]{2,4,3,0,1:T(8,128)(2,1)} async-done(((bf16[32,16,32,2,16]{2,4,3,0,1:T(8,128)(2,1)}), bf16[32,4,32,2,16]{2,4,3,0,1:T(8,128)(2,1)}) %reduce-scatter.3.cloned.1.call-update) | async-done | bytes 262160 | tf_op jit(solution)/shard_map/reduce_scatter | solution.py:95
  80.1 11.0 %all-gather.3.cloned.1.call-done = bf16[1,4,4,2,32,32,16]{4,6,5,3,2,1,0:T(8,128)(2,1)} async-done(((bf16[1,4,4,2,32,16,16]{4,6,5,3,2,1,0:T(8,128)(2,1)}), bf16[1,4,4,2,32,32,16]{4,6,5,3,2,1,0:T(8,128)(2,1)}) %all-gather.3.cloned.1.call-update) | async-done | bytes 1048592 | tf_op jit(solution)/shard_map/all_gather | solution.py:103
  91.1 4.5 %slice_bitcast_fusion = (bf16[4,4,32,32,16]{2,4,3,1,0:T(8,128)(2,1)}, bf16[4,4,32,32,16]{2,4,3,1,0:T(8,128)(2,1)S(1)}) fusion(bf16[4,4,2,32,32,16]{3,5,4,2,1,0:T(8,128)(2,1)} %bitcast.161), kind=kLoop, calls=%fused_computation.39 | loop fusion | bytes 2097152 | tf_op jit(solution)/shard_map/squeeze | solution.py:60
  95.6 4.5 %copy.45 = bf16[4,4,32,32,16]{3,2,4,1,0:T(8,128)(2,1)} copy(bf16[4,4,32,32,16]{2,4,3,1,0:T(8,128)(2,1)} %get-tuple-element.5) | data formatting | bytes 1048576 | tf_op jit(solution)/shard_map/squeeze | solution.py:60
  100.2 2.9 %copy.42 = bf16[4,4,32,32,16]{3,2,4,1,0:T(8,128)(2,1)} copy(bf16[4,4,32,32,16]{2,4,3,1,0:T(8,128)(2,1)S(1)} %get-tuple-element.6) | data formatting | bytes 1048576 | tf_op jit(solution)/shard_map/squeeze | solution.py:59
  106.2 2.3 fusion.37
  108.5 2.2 fusion.35
  110.7 2.3 fusion.41
  113.1 7.2 %all_gather.7 = bf16[4,16,32,2,16]{2,4,3,0,1:T(8,128)(2,1)S(1)} all-gather(bf16[4,4,32,2,16]{2,4,3,0,1:T(8,128)(2,1)S(1)} %pad_maximum_fusion), channel_id=1, replica_groups=mesh['gx'=4,'gy'=4,'col'=2] {'gy'}, dimensions={1}, use_global_device_ids=true | all-gather | bytes 163840 | tf_op jit(solution)/shard_map/all_gather | solution.py:106
  122.2 11.5 %fusion.13 = f32[32,32,128,32]{2,3,1,0:T(8,128)} fusion(bf16[1,32,32,32,128]{4,3,2,1,0:T(8,128)(2,1)} %param.6, bf16[1,32,32]{2,1,0:T(8,128)(2,1)S(1)} %copy-done), kind=kOutput, calls=%fused_computation.27 | convolution fusion | flops 268435456 | bytes 25167872 | tf_op jit(solution)/shard_map/oc,xycz->xyoz/dot_general | solution.py:125
  133.7 3.0 %collective-permute-done = bf16[4,16,32,2,16]{2,0,3,4,1:T(4,128)(2,1)S(1)} collective-permute-done((bf16[4,16,32,2,16]{2,0,3,4,1:T(4,128)(2,1)S(1)}, bf16[4,16,32,2,16]{2,0,3,4,1:T(4,128)(2,1)S(1)}, u32[]{:S(2)}, u32[]{:S(2)}) %collective-permute-start) | collective-permute-done | bytes 131104 | tf_op jit(solution)/shard_map/ppermute | solution.py:109
  136.9 14.9 %collective-permute-done.1 = bf16[4,16,32,2,16]{2,0,3,4,1:T(4,128)(2,1)S(1)} collective-permute-done((bf16[4,16,32,2,16]{2,0,3,4,1:T(4,128)(2,1)S(1)}, bf16[4,16,32,2,16]{2,0,3,4,1:T(4,128)(2,1)S(1)}, u32[]{:S(2)}, u32[]{:S(2)}) %collective-permute-start.1) | collective-permute-done | bytes 131104 | tf_op jit(solution)/shard_map/ppermute | solution.py:109
  151.9 14.2 %collective-permute-done.2 = bf16[4,16,32,2,16]{2,0,3,4,1:T(4,128)(2,1)S(1)} collective-permute-done((bf16[4,16,32,2,16]{2,0,3,4,1:T(4,128)(2,1)S(1)}, bf16[4,16,32,2,16]{2,0,3,4,1:T(4,128)(2,1)S(1)}, u32[]{:S(2)}, u32[]{:S(2)}) %collective-permute-start.2) | collective-permute-done | bytes 131104 | tf_op jit(solution)/shard_map/ppermute | solution.py:109
  166.1 12.3 %concatenate.15 = bf16[32,16,32,2,16]{2,0,3,4,1:T(8,128)(2,1)} concatenate(bf16[4,16,32,2,16]{2,0,3,4,1:T(4,128)(2,1)S(1)} %collective-permute-done.2, bf16[4,16,32,2,16]{2,0,3,4,1:T(4,128)(2,1)S(1)} %collective-permute-done.1, bf16[4,16,32,2,16]{2,0,3,4,1:T(4,128)(2,1)S(1)} %collective-permute-done, bf16[4,16,32,2,16]{2,0,3,4,1:T(4,128)(2,1)S(1)} %copy.30, ...), dimensions={0} | concatenate | bytes 2097152 | tf_op jit(solution)/shard_map/jit(_roll_dynamic)/concatenate | solution.py:110
  178.4 3.2 %convolution_bitcast_fusion = f32[32,16,32,2,16]{2,0,4,1,3:T(8,128)S(1)} fusion(bf16[32,16,32,2,16]{2,0,3,4,1:T(8,128)(2,1)} %concatenate.15, s32[]{:T(128)S(6)} %select_n.131, bf16[16,1,32,2]{2,0,1,3:T(8,128)(2,1)S(1)} %get-tuple-element.14, bf16[16,1,32,2]{2,0,1,3:T(8,128)(2,1)S(1)} %get-tuple-element.13), kind=kOutput, calls=%fused_computation.38 | convolution fusion | flops 33562624 | bytes 4198404 | tf_op jit(solution)/shard_map/jkcsz,jsxt->xkctz/dot_general | solution.py:113
  181.6 22.8 %fusion.12 = bf16[32,32,32,2,16]{2,1,4,0,3:T(8,128)(2,1)} fusion(f32[32,16,32,2,16]{2,0,4,1,3:T(8,128)S(1)} %convolution_bitcast_fusion, f32[16,1,32,2]{2,0,3,1:T(8,128)S(1)} %get-tuple-element.10, f32[16,1,32,2]{2,0,3,1:T(8,128)S(1)} %get-tuple-element.9), kind=kOutput, calls=%fused_computation.26 | convolution fusion | flops 403703808 | bytes 4202496 | tf_op jit(solution)/shard_map/xkcsz,ksyt->xyctz/dot_general | solution.py:116
  204.4 10.5 %copy.35 = bf16[32,32,32,2,16]{2,4,3,1,0:T(8,128)(2,1)} copy(bf16[32,32,32,2,16]{2,1,4,0,3:T(8,128)(2,1)} %fusion.12) | data formatting | bytes 4194304 | tf_op jit(solution)/shard_map/convert_element_type | solution.py:118
  214.9 14.5 %fusion.94 = (f32[32,32,128]{2,1,0:T(8,128)S(1)}, f32[32,32,32,128]{3,2,1,0:T(8,128)}) fusion(f32[32]{0:T(128)S(1)} %bitcast.164, f32[32,32,128,32]{2,3,1,0:T(8,128)} %fusion.13, bf16[32,32,32,32]{2,3,1,0:T(8,128)(2,1)} %bitcast.160, bf16[16,128]{1,0:T(8,128)(2,1)S(1)} %get-tuple-element.41, bf16[16,128]{1,0:T(8,128)(2,1)S(1)} %get-tuple-element.42), kind=kOutput, calls=%fused_computation.168 | convolution fusion | flops 285097984 | bytes 36184192 | tf_op jit(solution)/shard_map/dot_general | solution.py:119
  229.5 10.9 %multiply_reduce_fusion = f32[32,32,128]{2,1,0:T(8,128)S(1)} fusion(f32[32,32,32,128]{3,2,1,0:T(8,128)} %get-tuple-element.36, f32[32,32,128]{2,1,0:T(8,128)S(1)} %broadcast_multiply_fusion), kind=kLoop, calls=%fused_computation.23 | loop fusion | flops 12451840 | bytes 17825792 | tf_op jit(solution)/shard_map/reduce_sum | solution.py:69
  240.5 41.4 %fusion.21 = bf16[1,32,32,32,128]{4,3,2,1,0:T(8,128)(2,1)} fusion(f32[32]{0:T(128)S(1)} %bitcast.162, f32[32]{0:T(128)S(1)} %bitcast.163, f32[32,32,128]{2,1,0:T(8,128)S(1)} %add_rsqrt_fusion, f32[32,32,32,128]{3,2,1,0:T(8,128)} %get-tuple-element.36, f32[32,32,128]{2,1,0:T(8,128)S(1)} %broadcast_multiply_fusion), kind=kLoop, calls=%fused_computation.36 | loop fusion | flops 289406976 | bytes 26214656 | tf_op jit(solution)/shard_map/broadcast_in_dim | solution.py:129
  (40 shorter events, 9.3 us)
Async XLA Ops:
  7.4 114.9 %copy-start = (bf16[1,32,32]{2,1,0:T(8,128)(2,1)S(1)}, bf16[1,32,32]{2,1,0:T(8,128)(2,1)}, u32[]{:S(2)}) copy-start(bf16[1,32,32]{2,1,0:T(8,128)(2,1)} %param.8) | copy-start | bytes 6148
  7.4 69.8 %reduce-scatter.3.cloned.1.call-start = ((), (), s32[]{:S(2)}) async-start(), calls=%async_computation.2 | async-start | bytes 5242880 | tf_op jit(solution)/shard_map/reduce_scatter | solution.py:95
  29.7 61.4 %all-gather.3.cloned.1.call-start = ((), (), s32[]{:S(2)}) async-start(), calls=%async_computation.4 | async-start | bytes 6291456 | tf_op jit(solution)/shard_map/all_gather | solution.py:103
  30.3 72.8 %reduce-scatter.5.cloned.1.call-start = ((), (), s32[]{:S(2)}) async-start(), calls=%async_computation.3 | async-start | bytes 655360 | tf_op jit(solution)/shard_map/reduce_scatter | solution.py:99
  120.5 16.2 %collective-permute-start = (bf16[4,16,32,2,16]{2,0,3,4,1:T(4,128)(2,1)S(1)}, bf16[4,16,32,2,16]{2,0,3,4,1:T(4,128)(2,1)S(1)}, u32[]{:S(2)}, u32[]{:S(2)}) collective-permute-start(bf16[4,16,32,2,16]{2,0,3,4,1:T(4,128)(2,1)S(1)} %copy.30), channel_id=1, source_target_pairs={{0,8},{8,16},{16,24},{24,0},{1,9},{9,17},{17,25},{25,1},{2,10},{10... | collective-permute-start | bytes 393224 | tf_op jit(solution)/shard_map/ppermute | solution.py:109
  136.7 15.1 %collective-permute-start.1 = (bf16[4,16,32,2,16]{2,0,3,4,1:T(4,128)(2,1)S(1)}, bf16[4,16,32,2,16]{2,0,3,4,1:T(4,128)(2,1)S(1)}, u32[]{:S(2)}, u32[]{:S(2)}) collective-permute-start(bf16[4,16,32,2,16]{2,0,3,4,1:T(4,128)(2,1)S(1)} %collective-permute-done), channel_id=1, source_target_pairs={{0,8},{8,16},{16,24},{24,0},{1,9},{9,17},{17,25},{25,1},{2,10},{10... | collective-permute-start | bytes 393224 | tf_op jit(solution)/shard_map/ppermute | solution.py:109
  151.8 14.3 %collective-permute-start.2 = (bf16[4,16,32,2,16]{2,0,3,4,1:T(4,128)(2,1)S(1)}, bf16[4,16,32,2,16]{2,0,3,4,1:T(4,128)(2,1)S(1)}, u32[]{:S(2)}, u32[]{:S(2)}) collective-permute-start(bf16[4,16,32,2,16]{2,0,3,4,1:T(4,128)(2,1)S(1)} %collective-permute-done.1), channel_id=1, source_target_pairs={{0,8},{8,16},{16,24},{24,0},{1,9},{9,17},{17,25},{25,1},{2,10},{10... | collective-permute-start | bytes 393224 | tf_op jit(solution)/shard_map/ppermute | solution.py:109
  181.6 33.3 %copy-start.4 = (f32[1,32]{1,0:T(1,128)S(1)}, f32[1,32]{1,0:T(1,128)}, u32[]{:S(2)}) copy-start(f32[1,32]{1,0:T(1,128)} %param.9) | copy-start | bytes 388
  229.4 11.1 %copy-start.2 = (f32[1,32]{1,0:T(1,128)S(1)}, f32[1,32]{1,0:T(1,128)}, u32[]{:S(2)}) copy-start(f32[1,32]{1,0:T(1,128)} %param.11) | copy-start | bytes 388
  229.4 11.1 %copy-start.3 = (f32[1,32]{1,0:T(1,128)S(1)}, f32[1,32]{1,0:T(1,128)}, u32[]{:S(2)}) copy-start(f32[1,32]{1,0:T(1,128)} %param.10) | copy-start | bytes 388
  229.4 52.5 %copy-start.1 = (bf16[1,32,32]{2,1,0:T(8,128)(2,1)S(1)}, bf16[1,32,32]{2,1,0:T(8,128)(2,1)}, u32[]{:S(2)}) copy-start(bf16[1,32,32]{2,1,0:T(8,128)(2,1)} %param.8) | copy-start | bytes 6148
Sparse Core Ops, SparseCore 0:
  29.9 47.2 reduce-scatter.2
  80.2 21.8 reduce-scatter.4
Sparse Core Ops, SparseCore 1:
  31.8 59.3 all-gather.2
